TPU v7x, 32 devices: a whole 2x2x4 slice. The times are simulated.
32 devices in a mesh: rows: 4 (over z), cols: 2 (over x), slabs: 4 (over y, core).
Axes of the slice: x: 2, y: 2, z: 4, core: 2. Of those that a mesh axis runs over, the one named last changes fastest.
Arguments:
- pressure: float32 [512, 8, 128, 128], P('rows', 'cols', 'slabs'), may hold values from 0.5 to 2
- earlier: float32 [512, 8, 128, 128], P('rows', 'cols', 'slabs'), may hold values from 0.2 to 1.8
- speed_square: float32 [512, 8, 128, 128], P('rows', 'cols', 'slabs'), may hold values from 0.05 to 0.3
Outputs:
- scaled_field: float32 [512, 8, 128, 128], P('rows', 'cols', 'slabs')
- pressure_end: float32 [512, 8, 128, 128], P('rows', 'cols', 'slabs')
All inputs are finite; a program needn't handle non-finite values.
Results may differ from a plain program's by a relative error of at most 0.00002.
Values sent between devices are 32-bit elements; how exact they have to be, the bound alone decides.
A program may use at most 128 MiB of HBM per device.

v0:
```python
import functools

import jax
import jax.numpy as jnp
from jax import lax
from jax.experimental import pallas as pl
from jax.experimental.pallas import tpu as pltpu
from jax.sharding import PartitionSpec as P

STEPS = 3
GUESS = 1.0
EPS = 0.0001
MESH = pl.DeviceIdType.MESH
TILE = 8
LO, HI = 0, 1


def leapfrog(sizes, p_hbm, e_hbm, s_hbm, end, stat,
             even, odd, xh, yh, line,
             xs, xr, ys, yr, zs, zr, ls, lr, own):
    speed = end
    rows, cols, slabs = sizes
    planes, cells, depth = p_hbm.shape[0], p_hbm.shape[1], p_hbm.shape[2]
    tiles = depth // TILE
    body_planes = pl.ds(1, planes)
    row, col, slab = (lax.axis_index(name) for name in ("rows", "cols", "slabs"))

    def shifted(name, index, count, by):
        return {name: lax.rem(index + by + count, count)}

    x_to = (shifted("cols", col, cols, -1), shifted("cols", col, cols, 1))
    y_to = (shifted("slabs", slab, slabs, -1), shifted("slabs", slab, slabs, 1))
    z_to = (shifted("rows", row, rows, -1), shifted("rows", row, rows, 1))
    peers = [shifted("rows", row, rows, d) for d in range(1, rows)]

    loads = [
        pltpu.make_async_copy(p_hbm, even.at[body_planes], own.at[0]),
        pltpu.make_async_copy(e_hbm, odd.at[body_planes], own.at[1]),
        pltpu.make_async_copy(s_hbm, speed, own.at[2]),
    ]
    for load in loads:
        load.start()

    barrier = pltpu.get_barrier_semaphore()
    greeted = list(x_to) + list(y_to) + peers
    for device in greeted:
        pl.semaphore_signal(barrier, inc=1, device_id=device, device_id_type=MESH)
    pl.semaphore_wait(barrier, len(greeted))

    fields = (even, odd)
    count = float(planes * rows)

    def line_copies(cell, q):
        part = line.at[row, cell, q]
        return [remote(part, part, ls.at[cell, q, d], lr.at[cell, q, d], device)
                for d, device in enumerate(peers)]

    def remote(src, dst, send, recv, device):
        return pltpu.make_async_remote_copy(
            src_ref=src, dst_ref=dst, send_sem=send, recv_sem=recv,
            device_id=device, device_id_type=MESH,
        )

    def source(step):
        return p_hbm if step == 0 else fields[step % 2].at[body_planes]

    def x_copy(step, side, q):
        cell = 0 if side == LO else cells - 1
        part = pl.ds(q * TILE, TILE)
        return remote(source(step).at[:, cell, part, :], xh.at[step, 1 - side, :, part, :],
                      xs.at[step, side, q], xr.at[step, side, q], x_to[side])

    def y_copy(step, side):
        part = pl.ds(0 if side == LO else depth - TILE, TILE)
        return remote(source(step).at[:, :, part, :], yh.at[step, 1 - side],
                      ys.at[step, side], yr.at[step, side], y_to[side])

    def z_copy(step, side):
        src = p_hbm.at[0 if side == LO else planes - 1] if step == 0 else (
            fields[step % 2].at[1 if side == LO else planes])
        dst = fields[step % 2].at[planes + 1 if side == LO else 0]
        return remote(src, dst, zs.at[step, side], zr.at[step, side], z_to[side])

    def order(step):
        return (LO, HI) if step % 2 == 0 else (HI, LO)

    def update(step, cell, q, low, high):
        now, then = fields[step % 2], fields[(step + 1) % 2]
        part = pl.ds(q * TILE, TILE)
        index = lax.broadcasted_iota(jnp.int32, (TILE, TILE, 128), 1)
        last = step == STEPS - 1

        def block(b, sums):
            j = b * TILE
            here, padded = pl.ds(j, TILE), pl.ds(j + 1, TILE)
            mid = now[padded, cell, part, :]
            if q == 0:
                below = yh[step, LO, here, cell, TILE - 1:TILE, :]
            else:
                below = now[padded, cell, q * TILE - 1:q * TILE, :]
            if q == tiles - 1:
                above = yh[step, HI, here, cell, 0:1, :]
            else:
                above = now[padded, cell, (q + 1) * TILE:(q + 1) * TILE + 1, :]
            k_low = jnp.where(index == 0, below, pltpu.roll(mid, 1, 1))
            k_high = jnp.where(index == TILE - 1, above, pltpu.roll(mid, TILE - 1, 1))
            spread = (now[here, cell, part, :] + now[pl.ds(j + 2, TILE), cell, part, :]
                      + low(here, padded, part) + high(here, padded, part)
                      + k_low + k_high - 6.0 * mid)
            new = 2.0 * mid - then[padded, cell, part, :] + speed[here, cell, part, :] * spread
            if last:
                end[here, cell, part, :] = new
                moved = new - GUESS
                return sums[0] + jnp.sum(moved, axis=0), sums[1] + jnp.sum(moved * moved, axis=0)
            then[padded, cell, part, :] = new
            return sums

        zero = jnp.zeros((TILE, 128), jnp.float32)
        sums = lax.fori_loop(0, planes // TILE, block, (zero, zero) if last else 0)
        if last:
            line[row, cell, q, 0] = sums[0]
            line[row, cell, q, 1] = sums[1]
            for copy in line_copies(cell, q):
                copy.start()

    def edge(step, side, q):
        now = fields[step % 2]
        halo = lambda here, padded, part: xh[step, side, here, part, :]
        if side == LO:
            update(step, 0, q, halo, lambda here, padded, part: now[padded, 1, part, :])
        else:
            update(step, cells - 1, q, lambda here, padded, part: now[padded, cells - 2, part, :], halo)

    def interior(step):
        now = fields[step % 2]

        def at(cell, carry):
            for q in range(tiles):
                update(step, cell, q,
                       lambda here, padded, part: now[padded, cell - 1, part, :],
                       lambda here, padded, part: now[padded, cell + 1, part, :])
            return carry

        lax.fori_loop(1, cells - 1, at, 0)

    def settle(cell):
        for q in range(tiles):
            for copy in line_copies(cell, q):
                copy.wait()
            total, square = line[0, cell, q, 0], line[0, cell, q, 1]
            for r in range(1, rows):
                total, square = total + line[r, cell, q, 0], square + line[r, cell, q, 1]
            shift = total / count
            part = pl.ds(q * TILE, TILE)
            stat[0, cell, part, :] = GUESS + shift
            stat[1, cell, part, :] = lax.rsqrt(square / count - shift * shift + EPS)

    for side in order(0):
        for q in range(tiles):
            x_copy(0, side, q).start()
    for side in (LO, HI):
        z_copy(0, side).start()
        y_copy(0, side).start()
    for load in loads:
        load.wait()

    for step in range(STEPS):
        if step >= 1:
            for side in order(step - 1):
                z_copy(step - 1, side).wait_send()
                y_copy(step - 1, side).wait_send()
                for q in range(tiles):
                    x_copy(step - 1, side, q).wait_send()
        for side in (LO, HI):
            z_copy(step, side).wait_recv()
            y_copy(step, side).wait_recv()
        interior(step)
        for side in order(step):
            for q in range(tiles):
                x_copy(step, side, q).wait_recv()
                edge(step, 1 - side, q)
                if step < STEPS - 1:
                    x_copy(step + 1, 1 - side, q).start()
            if step == STEPS - 1 and side == order(step)[0]:
                for cell in range(1, cells - 1):
                    settle(cell)
        if step < STEPS - 1:
            for side in (LO, HI):
                z_copy(step + 1, side).start()
                y_copy(step + 1, side).start()

    for side in order(STEPS - 1):
        z_copy(STEPS - 1, side).wait_send()
        y_copy(STEPS - 1, side).wait_send()
        for q in range(tiles):
            x_copy(STEPS - 1, side, q).wait_send()

    for side in order(STEPS - 1):
        settle(0 if side == HI else cells - 1)


def rescale(p_ref, stat_ref, scaled_hbm, end_hbm, scaled, end_sem, scaled_sem):
    planes, parts = p_ref.shape[0], end_sem.shape[0]
    each = planes // parts
    copies = []
    for c in range(parts):
        part = pl.ds(c * each, each)
        copies.append((pltpu.make_async_copy(p_ref.at[part], end_hbm.at[part], end_sem.at[c]),
                       pltpu.make_async_copy(scaled.at[part], scaled_hbm.at[part], scaled_sem.at[c])))

    for c in range(parts):
        copies[c][0].start()

        def plane(j, carry):
            scaled[j] = (p_ref[j] - stat_ref[0]) * stat_ref[1]
            return carry

        lax.fori_loop(c * each, (c + 1) * each, plane, 0, unroll=2)
        copies[c][1].start()
    for pair in copies:
        for copy in pair:
            copy.wait()


def shards(sizes, pressure, earlier, speed_square):
    rows = sizes[0]
    planes, cells, depth, members = pressure.shape
    tiles = depth // TILE
    any_space = pl.BlockSpec(memory_space=pl.ANY)
    dma = pltpu.SemaphoreType.DMA
    vmem_space = pl.BlockSpec(memory_space=pltpu.VMEM)
    end, stat = pl.pallas_call(
        functools.partial(leapfrog, sizes),
        out_shape=(
            pltpu.VMEM(pressure.shape, jnp.float32),
            pltpu.VMEM((2, cells, depth, members), jnp.float32),
        ),
        in_specs=[any_space] * 3,
        out_specs=(vmem_space, vmem_space),
        scratch_shapes=[
            pltpu.VMEM((planes + 2, cells, depth, members), jnp.float32),
            pltpu.VMEM((planes + 2, cells, depth, members), jnp.float32),
            pltpu.VMEM((STEPS, 2, planes, depth, members), jnp.float32),
            pltpu.VMEM((STEPS, 2, planes, cells, TILE, members), jnp.float32),
            pltpu.VMEM((rows, cells, tiles, 2, TILE, members), jnp.float32),
            dma((STEPS, 2, tiles)), dma((STEPS, 2, tiles)),
            dma((STEPS, 2)), dma((STEPS, 2)),
            dma((STEPS, 2)), dma((STEPS, 2)),
            dma((cells, tiles, rows - 1)), dma((cells, tiles, rows - 1)),
            dma((3,)),
        ],
        compiler_params=pltpu.CompilerParams(
            collective_id=0, has_side_effects=True, vmem_limit_bytes=46 * 1024 * 1024
        ),
    )(pressure, earlier, speed_square)

    parts = 8
    return pl.pallas_call(
        rescale,
        out_shape=(jax.ShapeDtypeStruct(pressure.shape, jnp.float32),) * 2,
        in_specs=[vmem_space, vmem_space],
        out_specs=(any_space, any_space),
        scratch_shapes=[pltpu.VMEM(pressure.shape, jnp.float32), dma((parts,)), dma((parts,))],
        compiler_params=pltpu.CompilerParams(vmem_limit_bytes=24 * 1024 * 1024),
    )(end, stat)


def solution(mesh):
    spec = P("rows", "cols", "slabs", None)
    sizes = tuple(mesh.shape[name] for name in ("rows", "cols", "slabs"))
    return jax.shard_map(functools.partial(shards, sizes), mesh=mesh,
                         in_specs=(spec,) * 3, out_specs=(spec,) * 2, check_vma=False)
```

profile of v0, /device:TPU:1, one launch (start us, length us, event | category | flops | bytes accessed | tf_op | source)
XLA Modules:
  0.0 288.0 jit_solution(17567628987237482989)
XLA Ops:
  0.6 281.4 %shard_map.50 = (f32[128,4,32,128]{3,2,1,0:T(8,128)S(1)}, f32[2,4,32,128]{3,2,1,0:T(8,128)S(1)}) custom-call(f32[128,4,32,128]{3,2,1,0:T(8,128)} %p_hbm.1, f32[128,4,32,128]{3,2,1,0:T(8,128)} %e_hbm.1, f32[128,4,32,128]{3,2,1,0:T(8,128)} %s_hbm.1), custom_call_target="tpu_custom_call" | custom-call | tf_op jit(solution)/shard_map/pallas_call | solution.py:232
  282.0 6.0 %shard_map.51 = (f32[128,4,32,128]{3,2,1,0:T(8,128)}, f32[128,4,32,128]{3,2,1,0:T(8,128)}) custom-call(f32[128,4,32,128]{3,2,1,0:T(8,128)S(1)} %get-tuple-element.4.p_ref, f32[2,4,32,128]{3,2,1,0:T(8,128)S(1)} %get-tuple-element.5.stat_ref), custom_call_target="tpu_custom_call" | custom-call | tf_op jit(solution)/shard_map/pallas_call | solution.py:258
where the time goes:
time: 289 us; the launch traced here: 288 us
  Pallas kernels  287 us (99%)
    pallas_call x1, Pallas kernels, shards(): pl.pallas_call(functools.partial(leapfrog, sizes), out_shape=(pltpu.VMEM(...  281 us
    pallas_call x1, Pallas kernels, shards(): pl.pallas_call(rescale, out_shape=(jax.ShapeDtypeStruct(pressure.shape, j...  5.96 us

commit v1 on v0

--- a/solution.py
+++ b/solution.py
@@ -12,12 +12,13 @@
 EPS = 0.0001
 MESH = pl.DeviceIdType.MESH
 TILE = 8
+PIECES = 4
 LO, HI = 0, 1
 
 
 def leapfrog(sizes, p_hbm, e_hbm, s_hbm, end, stat,
              even, odd, xh, yh, line,
-             xs, xr, ys, yr, zs, zr, ls, lr, own):
+             xs, xr, ps, pr, ys, yr, zs, zr, ls, lr, own):
     speed = end
     rows, cols, slabs = sizes
     planes, cells, depth = p_hbm.shape[0], p_hbm.shape[1], p_hbm.shape[2]
@@ -38,9 +39,6 @@
         pltpu.make_async_copy(e_hbm, odd.at[body_planes], own.at[1]),
         pltpu.make_async_copy(s_hbm, speed, own.at[2]),
     ]
-    for load in loads:
-        load.start()
-
     barrier = pltpu.get_barrier_semaphore()
     greeted = list(x_to) + list(y_to) + peers
     for device in greeted:
@@ -70,6 +68,18 @@
         return remote(source(step).at[:, cell, part, :], xh.at[step, 1 - side, :, part, :],
                       xs.at[step, side, q], xr.at[step, side, q], x_to[side])
 
+    def x_piece(side, piece):
+        cell = 0 if side == LO else cells - 1
+        q = tiles - 1
+        here, part = pl.ds(piece * (planes // PIECES), planes // PIECES), pl.ds(q * TILE, TILE)
+        return remote(source(STEPS - 1).at[here, cell, part, :], xh.at[STEPS - 1, 1 - side, here, part, :],
+                      ps.at[piece], pr.at[piece], x_to[side])
+
+    def x_copies(step, side, q):
+        if step == STEPS - 1 and side == order(step)[1] and q == tiles - 1:
+            return [x_piece(side, piece) for piece in range(PIECES)]
+        return [x_copy(step, side, q)]
+
     def y_copy(step, side):
         part = pl.ds(0 if side == LO else depth - TILE, TILE)
         return remote(source(step).at[:, :, part, :], yh.at[step, 1 - side],
@@ -84,7 +94,7 @@
     def order(step):
         return (LO, HI) if step % 2 == 0 else (HI, LO)
 
-    def update(step, cell, q, low, high):
+    def update(step, cell, q, low, high, copies=()):
         now, then = fields[step % 2], fields[(step + 1) % 2]
         part = pl.ds(q * TILE, TILE)
         index = lax.broadcasted_iota(jnp.int32, (TILE, TILE, 128), 1)
@@ -116,20 +126,29 @@
             return sums
 
         zero = jnp.zeros((TILE, 128), jnp.float32)
-        sums = lax.fori_loop(0, planes // TILE, block, (zero, zero) if last else 0)
+        sums = (zero, zero) if last else 0
+        count_of = max(len(copies), 1)
+        blocks = planes // TILE // count_of
+        for i in range(count_of):
+            if copies:
+                copies[i].wait_recv()
+            sums = lax.fori_loop(i * blocks, (i + 1) * blocks, block, sums)
         if last:
             line[row, cell, q, 0] = sums[0]
             line[row, cell, q, 1] = sums[1]
             for copy in line_copies(cell, q):
                 copy.start()
 
-    def edge(step, side, q):
+    def edge(step, side, q, copies):
         now = fields[step % 2]
         halo = lambda here, padded, part: xh[step, side, here, part, :]
         if side == LO:
-            update(step, 0, q, halo, lambda here, padded, part: now[padded, 1, part, :])
+            update(step, 0, q, halo, lambda here, padded, part: now[padded, 1, part, :], copies)
         else:
-            update(step, cells - 1, q, lambda here, padded, part: now[padded, cells - 2, part, :], halo)
+            update(step, cells - 1, q, lambda here, padded, part: now[padded, cells - 2, part, :], halo, copies)
+
+    def edge_cell(side):
+        return 0 if side == LO else cells - 1
 
     def interior(step):
         now = fields[step % 2]
@@ -143,8 +162,8 @@
 
         lax.fori_loop(1, cells - 1, at, 0)
 
-    def settle(cell):
-        for q in range(tiles):
+    def settle(cell, parts):
+        for q in parts:
             for copy in line_copies(cell, q):
                 copy.wait()
             total, square = line[0, cell, q, 0], line[0, cell, q, 1]
@@ -157,10 +176,13 @@
 
     for side in order(0):
         for q in range(tiles):
-            x_copy(0, side, q).start()
+            for copy in x_copies(0, side, q):
+                copy.start()
     for side in (LO, HI):
         z_copy(0, side).start()
         y_copy(0, side).start()
+    for load in loads:
+        load.start()
     for load in loads:
         load.wait()
 
@@ -170,20 +192,28 @@
                 z_copy(step - 1, side).wait_send()
                 y_copy(step - 1, side).wait_send()
                 for q in range(tiles):
-                    x_copy(step - 1, side, q).wait_send()
+                    for copy in x_copies(step - 1, side, q):
+                        copy.wait_send()
         for side in (LO, HI):
             z_copy(step, side).wait_recv()
             y_copy(step, side).wait_recv()
         interior(step)
-        for side in order(step):
+        first, second = order(step)
+        for side in (first, second):
             for q in range(tiles):
-                x_copy(step, side, q).wait_recv()
-                edge(step, 1 - side, q)
+                edge(step, 1 - side, q, x_copies(step, side, q))
                 if step < STEPS - 1:
-                    x_copy(step + 1, 1 - side, q).start()
-            if step == STEPS - 1 and side == order(step)[0]:
-                for cell in range(1, cells - 1):
-                    settle(cell)
+                    for copy in x_copies(step + 1, 1 - side, q):
+                        copy.start()
+                elif side == first and q == 0:
+                    for cell in range(1, cells - 1):
+                        settle(cell, range(tiles))
+                elif side == first:
+                    settle(edge_cell(1 - first), [q - 1])
+                elif q == 0:
+                    settle(edge_cell(1 - first), [tiles - 1])
+                else:
+                    settle(edge_cell(1 - second), [q - 1])
         if step < STEPS - 1:
             for side in (LO, HI):
                 z_copy(step + 1, side).start()
@@ -193,10 +223,10 @@
         z_copy(STEPS - 1, side).wait_send()
         y_copy(STEPS - 1, side).wait_send()
         for q in range(tiles):
-            x_copy(STEPS - 1, side, q).wait_send()
-
-    for side in order(STEPS - 1):
-        settle(0 if side == HI else cells - 1)
+            for copy in x_copies(STEPS - 1, side, q):
+                copy.wait_send()
+
+    settle(edge_cell(1 - order(STEPS - 1)[1]), [tiles - 1])
 
 
 def rescale(p_ref, stat_ref, scaled_hbm, end_hbm, scaled, end_sem, scaled_sem):
@@ -243,7 +273,7 @@
             pltpu.VMEM((STEPS, 2, planes, depth, members), jnp.float32),
             pltpu.VMEM((STEPS, 2, planes, cells, TILE, members), jnp.float32),
             pltpu.VMEM((rows, cells, tiles, 2, TILE, members), jnp.float32),
-            dma((STEPS, 2, tiles)), dma((STEPS, 2, tiles)),
+            dma((STEPS, 2, tiles)), dma((STEPS, 2, tiles)), dma((PIECES,)), dma((PIECES,)),
             dma((STEPS, 2)), dma((STEPS, 2)),
             dma((STEPS, 2)), dma((STEPS, 2)),
             dma((cells, tiles, rows - 1)), dma((cells, tiles, rows - 1)),

time: 289 us -> 289 us (level)
  no operation moved by 1% of the time
where the time goes in v1:
time: 289 us; the launch traced here: 288 us
  Pallas kernels  287 us (99%)
    pallas_call x1, Pallas kernels, shards(): pl.pallas_call(functools.partial(leapfrog, sizes), out_shape=(pltpu.VMEM(...  281 us
    pallas_call x1, Pallas kernels, shards(): pl.pallas_call(rescale, out_shape=(jax.ShapeDtypeStruct(pressure.shape, j...  5.96 us

profile of v1, /device:TPU:1, one launch (start us, length us, event | category | flops | bytes accessed | tf_op | source)
XLA Modules:
  0.0 287.7 jit_solution(8878596095100038971)
XLA Ops:
  0.6 281.1 %shard_map.50 = (f32[128,4,32,128]{3,2,1,0:T(8,128)S(1)}, f32[2,4,32,128]{3,2,1,0:T(8,128)S(1)}) custom-call(f32[128,4,32,128]{3,2,1,0:T(8,128)} %p_hbm.1, f32[128,4,32,128]{3,2,1,0:T(8,128)} %e_hbm.1, f32[128,4,32,128]{3,2,1,0:T(8,128)} %s_hbm.1), custom_call_target="tpu_custom_call" | custom-call | tf_op jit(solution)/shard_map/pallas_call | solution.py:262
  281.7 6.0 %shard_map.51 = (f32[128,4,32,128]{3,2,1,0:T(8,128)}, f32[128,4,32,128]{3,2,1,0:T(8,128)}) custom-call(f32[128,4,32,128]{3,2,1,0:T(8,128)S(1)} %get-tuple-element.4.p_ref, f32[2,4,32,128]{3,2,1,0:T(8,128)S(1)} %get-tuple-element.5.stat_ref), custom_call_target="tpu_custom_call" | custom-call | tf_op jit(solution)/shard_map/pallas_call | solution.py:288

commit v2 on v1

v2 whole, which is shorter than its diff:
```python
import functools

import jax
import jax.numpy as jnp
from jax import lax
from jax.experimental import pallas as pl
from jax.experimental.pallas import tpu as pltpu
from jax.sharding import PartitionSpec as P

STEPS = 3
GUESS = 1.0
EPS = 0.0001
MESH = pl.DeviceIdType.MESH
TILE = 8
PIECES = 4
PARTS = 8
LO, HI = 0, 1


def leapfrog(sizes, p_hbm, e_hbm, s_hbm, end, stat,
             even, odd, xh, yh, line,
             xs, xr, xp, ys, yr, zs, zr, ls, lr, own):
    speed = end
    rows, cols, slabs = sizes
    planes, cells, depth = p_hbm.shape[0], p_hbm.shape[1], p_hbm.shape[2]
    tiles = depth // TILE
    body_planes = pl.ds(1, planes)
    row, col, slab = (lax.axis_index(name) for name in ("rows", "cols", "slabs"))

    def shifted(name, index, count, by):
        return {name: lax.rem(index + by + count, count)}

    x_to = (shifted("cols", col, cols, -1), shifted("cols", col, cols, 1))
    y_to = (shifted("slabs", slab, slabs, -1), shifted("slabs", slab, slabs, 1))
    z_to = (shifted("rows", row, rows, -1), shifted("rows", row, rows, 1))
    peers = [shifted("rows", row, rows, d) for d in range(1, rows)]

    loads = [
        pltpu.make_async_copy(p_hbm, even.at[body_planes], own.at[0]),
        pltpu.make_async_copy(e_hbm, odd.at[body_planes], own.at[1]),
        pltpu.make_async_copy(s_hbm, speed, own.at[2]),
    ]
    barrier = pltpu.get_barrier_semaphore()
    near = y_to + z_to

    def greet(devices):
        for device in devices:
            pl.semaphore_signal(barrier, inc=1, device_id=device, device_id_type=MESH)

    colored = rows % 2 == 0 and slabs % 2 == 0
    color = lax.rem(row + slab, 2)
    greet(x_to)
    if colored:
        pl.semaphore_wait(barrier, len(x_to) + len(near) * color)
        greet(near)
    else:
        greet(near)
        pl.semaphore_wait(barrier, len(x_to) + len(near))

    fields = (even, odd)
    count = float(planes * rows)

    def order(step):
        return (LO, HI) if step % 2 == 0 else (HI, LO)

    def edge_cell(side):
        return 0 if side == LO else cells - 1

    early, late = (edge_cell(1 - side) for side in order(STEPS - 1))
    groups = [
        (pl.ds(1, cells - 2), slice(None), [(c, q) for c in range(1, cells - 1) for q in range(tiles)]),
        (early, slice(None), [(early, q) for q in range(tiles)]),
        (late, pl.ds(0, tiles - 1), [(late, q) for q in range(tiles - 1)]),
        (late, tiles - 1, [(late, tiles - 1)]),
    ]

    def line_copy(group, d):
        part = line.at[row, groups[group][0], groups[group][1]]
        return remote(part, part, ls.at[d], lr.at[group, d], peers[d])

    def send_lines(group):
        for d in range(rows - 1):
            if group > 0:
                line_copy(group - 1, d).wait_send()
            line_copy(group, d).start()

    def remote(src, dst, send, recv, device):
        return pltpu.make_async_remote_copy(
            src_ref=src, dst_ref=dst, send_sem=send, recv_sem=recv,
            device_id=device, device_id_type=MESH,
        )

    def source(step):
        return p_hbm if step == 0 else fields[step % 2].at[body_planes]

    def x_part(step, side, here, part, recv):
        return remote(source(step).at[here, edge_cell(side), part, :], xh.at[step, 1 - side, here, part, :],
                      xs.at[step % 2, side], recv, x_to[side])

    def x_copies(step, side, q):
        part = pl.ds(q * TILE, TILE)
        if step == STEPS - 1 and side == order(step)[1] and q == tiles - 1:
            each = planes // PIECES
            return [x_part(step, side, pl.ds(piece * each, each), part, xp.at[piece]) for piece in range(PIECES)]
        return [x_part(step, side, slice(None), part, xr.at[step % 2, side, q])]

    def x_sent(step, side):
        x_part(step, side, slice(None), slice(None), xp.at[0]).wait_send()

    def y_copy(step, side):
        part = pl.ds(0 if side == LO else depth - TILE, TILE)
        return remote(source(step).at[:, :, part, :], yh.at[step, 1 - side],
                      ys.at[step % 2, side], yr.at[step % 2, side], y_to[side])

    def z_copy(step, side):
        src = p_hbm.at[0 if side == LO else planes - 1] if step == 0 else (
            fields[step % 2].at[1 if side == LO else planes])
        dst = fields[step % 2].at[planes + 1 if side == LO else 0]
        return remote(src, dst, zs.at[step % 2, side], zr.at[step % 2, side], z_to[side])

    def update(step, cell, q, low, high, copies=(), before_last=None):
        now, then = fields[step % 2], fields[(step + 1) % 2]
        part = pl.ds(q * TILE, TILE)
        index = lax.broadcasted_iota(jnp.int32, (TILE, TILE, 128), 1)
        last = step == STEPS - 1

        def block(b, sums):
            j = b * TILE
            here, padded = pl.ds(j, TILE), pl.ds(j + 1, TILE)
            mid = now[padded, cell, part, :]
            if q == 0:
                below = yh[step, LO, here, cell, TILE - 1:TILE, :]
            else:
                below = now[padded, cell, q * TILE - 1:q * TILE, :]
            if q == tiles - 1:
                above = yh[step, HI, here, cell, 0:1, :]
            else:
                above = now[padded, cell, (q + 1) * TILE:(q + 1) * TILE + 1, :]
            k_low = jnp.where(index == 0, below, pltpu.roll(mid, 1, 1))
            k_high = jnp.where(index == TILE - 1, above, pltpu.roll(mid, TILE - 1, 1))
            spread = (now[here, cell, part, :] + now[pl.ds(j + 2, TILE), cell, part, :]
                      + low(here, padded, part) + high(here, padded, part)
                      + k_low + k_high - 6.0 * mid)
            new = 2.0 * mid - then[padded, cell, part, :] + speed[here, cell, part, :] * spread
            if last:
                end[here, cell, part, :] = new
                moved = new - GUESS
                return sums[0] + jnp.sum(moved, axis=0), sums[1] + jnp.sum(moved * moved, axis=0)
            then[padded, cell, part, :] = new
            return sums

        zero = jnp.zeros((TILE, 128), jnp.float32)
        sums = (zero, zero) if last else 0
        count_of = max(len(copies), 1)
        blocks = planes // TILE // count_of
        for i in range(count_of):
            if before_last is not None and i == count_of - 1:
                before_last()
            if copies:
                copies[i].wait_recv()
            sums = lax.fori_loop(i * blocks, (i + 1) * blocks, block, sums)
        if last:
            line[row, cell, q, 0] = sums[0]
            line[row, cell, q, 1] = sums[1]

    def edge(step, side, q, copies, before_last):
        now = fields[step % 2]
        halo = lambda here, padded, part: xh[step, side, here, part, :]
        if side == LO:
            update(step, 0, q, halo, lambda here, padded, part: now[padded, 1, part, :], copies, before_last)
        else:
            update(step, cells - 1, q, lambda here, padded, part: now[padded, cells - 2, part, :], halo, copies, before_last)

    def interior(step):
        now = fields[step % 2]

        def at(cell, carry):
            for q in range(tiles):
                update(step, cell, q,
                       lambda here, padded, part: now[padded, cell - 1, part, :],
                       lambda here, padded, part: now[padded, cell + 1, part, :])
            return carry

        lax.fori_loop(1, cells - 1, at, 0)

    def settle(group):
        for d in range(rows - 1):
            line_copy(group, d).wait_recv()
        for cell, q in groups[group][2]:
            total, square = line[0, cell, q, 0], line[0, cell, q, 1]
            for r in range(1, rows):
                total, square = total + line[r, cell, q, 0], square + line[r, cell, q, 1]
            shift = total / count
            part = pl.ds(q * TILE, TILE)
            stat[0, cell, part, :] = GUESS + shift
            stat[1, cell, part, :] = lax.rsqrt(square / count - shift * shift + EPS)

    for side in order(0):
        for q in range(tiles):
            for copy in x_copies(0, side, q):
                copy.start()
    if colored:
        @pl.when(color == 0)
        def _():
            pl.semaphore_wait(barrier, len(near))

    for side in (LO, HI):
        z_copy(0, side).start()
        y_copy(0, side).start()
    for load in loads:
        load.start()
    for load in loads:
        load.wait()

    for step in range(STEPS):
        if step >= 1:
            for side in order(step - 1):
                z_copy(step - 1, side).wait_send()
                y_copy(step - 1, side).wait_send()
                x_sent(step - 1, side)
        for side in (LO, HI):
            z_copy(step, side).wait_recv()
            y_copy(step, side).wait_recv()
        interior(step)
        if step == STEPS - 1:
            send_lines(0)
        first, second = order(step)
        for side in (first, second):
            for q in range(tiles):
                final = step == STEPS - 1
                hook = functools.partial(settle, 2) if final and side == second and q == tiles - 1 else None
                edge(step, 1 - side, q, x_copies(step, side, q), hook)
                if not final:
                    for copy in x_copies(step + 1, 1 - side, q):
                        copy.start()
                elif side == first:
                    if q == 0:
                        settle(0)
                    if q == tiles - 1:
                        send_lines(1)
                else:
                    if q == 0:
                        settle(1)
                    if q >= tiles - 2:
                        send_lines(q - tiles + 4)
        if step < STEPS - 1:
            for side in (LO, HI):
                z_copy(step + 1, side).start()
                y_copy(step + 1, side).start()

    for side in order(STEPS - 1):
        z_copy(STEPS - 1, side).wait_send()
        y_copy(STEPS - 1, side).wait_send()
        x_sent(STEPS - 1, side)

    settle(3)
    for d in range(rows - 1):
        line_copy(3, d).wait_send()


def rescale(p_ref, stat_ref, scaled_hbm, end_hbm, scaled, end_sem, scaled_sem):
    planes = p_ref.shape[0]
    each = planes // PARTS
    parts = [pl.ds(c * each, each) for c in range(PARTS)]
    for part in parts:
        pltpu.make_async_copy(p_ref.at[part], end_hbm.at[part], end_sem).start()

    def plane(j, carry):
        scaled[j] = (p_ref[j] - stat_ref[0]) * stat_ref[1]
        return carry

    for c, part in enumerate(parts):
        lax.fori_loop(c * each, (c + 1) * each, plane, 0, unroll=2)
        pltpu.make_async_copy(scaled.at[part], scaled_hbm.at[part], scaled_sem).start()
    pltpu.make_async_copy(p_ref, end_hbm, end_sem).wait()
    pltpu.make_async_copy(scaled, scaled_hbm, scaled_sem).wait()


def shards(sizes, pressure, earlier, speed_square):
    rows = sizes[0]
    planes, cells, depth, members = pressure.shape
    tiles = depth // TILE
    any_space = pl.BlockSpec(memory_space=pl.ANY)
    dma = pltpu.SemaphoreType.DMA
    vmem_space = pl.BlockSpec(memory_space=pltpu.VMEM)
    end, stat = pl.pallas_call(
        functools.partial(leapfrog, sizes),
        out_shape=(
            pltpu.VMEM(pressure.shape, jnp.float32),
            pltpu.VMEM((2, cells, depth, members), jnp.float32),
        ),
        in_specs=[any_space] * 3,
        out_specs=(vmem_space, vmem_space),
        scratch_shapes=[
            pltpu.VMEM((planes + 2, cells, depth, members), jnp.float32),
            pltpu.VMEM((planes + 2, cells, depth, members), jnp.float32),
            pltpu.VMEM((STEPS, 2, planes, depth, members), jnp.float32),
            pltpu.VMEM((STEPS, 2, planes, cells, TILE, members), jnp.float32),
            pltpu.VMEM((rows, cells, tiles, 2, TILE, members), jnp.float32),
            dma((2, 2)), dma((2, 2, tiles)), dma((PIECES,)),
            dma((2, 2)), dma((2, 2)),
            dma((2, 2)), dma((2, 2)),
            dma((rows - 1,)), dma((4, rows - 1)),
            dma((3,)),
        ],
        compiler_params=pltpu.CompilerParams(
            collective_id=0, has_side_effects=True, vmem_limit_bytes=46 * 1024 * 1024
        ),
    )(pressure, earlier, speed_square)

    return pl.pallas_call(
        rescale,
        out_shape=(jax.ShapeDtypeStruct(pressure.shape, jnp.float32),) * 2,
        in_specs=[vmem_space, vmem_space],
        out_specs=(any_space, any_space),
        scratch_shapes=[pltpu.VMEM(pressure.shape, jnp.float32), dma, dma],
        compiler_params=pltpu.CompilerParams(vmem_limit_bytes=24 * 1024 * 1024),
    )(end, stat)


def solution(mesh):
    spec = P("rows", "cols", "slabs", None)
    sizes = tuple(mesh.shape[name] for name in ("rows", "cols", "slabs"))
    return jax.shard_map(functools.partial(shards, sizes), mesh=mesh,
                         in_specs=(spec,) * 3, out_specs=(spec,) * 2, check_vma=False)
```

time: 289 us -> 286 us (0.990)
  Pallas kernels: 287 us -> 284 us
where the time goes in v2:
time: 286 us; the launch traced here: 285 us
  Pallas kernels  284 us (99%)
    pallas_call x1, Pallas kernels, shards(): pl.pallas_call(functools.partial(leapfrog, sizes), out_shape=(pltpu.VMEM(...  279 us
    pallas_call x1, Pallas kernels, shards(): pl.pallas_call(rescale, out_shape=(jax.ShapeDtypeStruct(pressure.shape, j...  5.84 us

profile of v2, /device:TPU:1, one launch (start us, length us, event | category | flops | bytes accessed | tf_op | source)
XLA Modules:
  0.0 285.0 jit_solution(3511435926030714245)
XLA Ops:
  0.6 278.6 %shard_map.50 = (f32[128,4,32,128]{3,2,1,0:T(8,128)S(1)}, f32[2,4,32,128]{3,2,1,0:T(8,128)S(1)}) custom-call(f32[128,4,32,128]{3,2,1,0:T(8,128)} %p_hbm.1, f32[128,4,32,128]{3,2,1,0:T(8,128)} %e_hbm.1, f32[128,4,32,128]{3,2,1,0:T(8,128)} %s_hbm.1), custom_call_target="tpu_custom_call" | custom-call | tf_op jit(solution)/shard_map/pallas_call | solution.py:286
  279.2 5.8 %shard_map.51 = (f32[128,4,32,128]{3,2,1,0:T(8,128)}, f32[128,4,32,128]{3,2,1,0:T(8,128)}) custom-call(f32[128,4,32,128]{3,2,1,0:T(8,128)S(1)} %get-tuple-element.4.p_ref, f32[2,4,32,128]{3,2,1,0:T(8,128)S(1)} %get-tuple-element.5.stat_ref), custom_call_target="tpu_custom_call" | custom-call | tf_op jit(solution)/shard_map/pallas_call | solution.py:311

commit v3 on v2

--- a/solution.py
+++ b/solution.py
@@ -19,7 +19,7 @@
 
 def leapfrog(sizes, p_hbm, e_hbm, s_hbm, end, stat,
              even, odd, xh, yh, line,
-             xs, xr, xp, ys, yr, zs, zr, ls, lr, own):
+             xs, xr, xp, ys, yr, zs, zr, ls, lr, own, heard):
     speed = end
     rows, cols, slabs = sizes
     planes, cells, depth = p_hbm.shape[0], p_hbm.shape[1], p_hbm.shape[2]
@@ -47,12 +47,13 @@
         for device in devices:
             pl.semaphore_signal(barrier, inc=1, device_id=device, device_id_type=MESH)
 
-    colored = rows % 2 == 0 and slabs % 2 == 0
-    color = lax.rem(row + slab, 2)
+    paired = slabs % 2 == 0
+    early = lax.rem(slab, 2) == 0
     greet(x_to)
-    if colored:
-        pl.semaphore_wait(barrier, len(x_to) + len(near) * color)
-        greet(near)
+    if paired:
+        pl.when(jnp.logical_not(early))(lambda: greet(z_to))
+        pl.semaphore_wait(barrier, len(x_to) + len(near) * lax.rem(slab, 2))
+        greet(y_to)
     else:
         greet(near)
         pl.semaphore_wait(barrier, len(x_to) + len(near))
@@ -66,12 +67,12 @@
     def edge_cell(side):
         return 0 if side == LO else cells - 1
 
-    early, late = (edge_cell(1 - side) for side in order(STEPS - 1))
+    sooner, later = (edge_cell(1 - side) for side in order(STEPS - 1))
     groups = [
         (pl.ds(1, cells - 2), slice(None), [(c, q) for c in range(1, cells - 1) for q in range(tiles)]),
-        (early, slice(None), [(early, q) for q in range(tiles)]),
-        (late, pl.ds(0, tiles - 1), [(late, q) for q in range(tiles - 1)]),
-        (late, tiles - 1, [(late, tiles - 1)]),
+        (sooner, slice(None), [(sooner, q) for q in range(tiles)]),
+        (later, pl.ds(0, tiles - 1), [(later, q) for q in range(tiles - 1)]),
+        (later, tiles - 1, [(later, tiles - 1)]),
     ]
 
     def line_copy(group, d):
@@ -110,13 +111,13 @@
     def y_copy(step, side):
         part = pl.ds(0 if side == LO else depth - TILE, TILE)
         return remote(source(step).at[:, :, part, :], yh.at[step, 1 - side],
-                      ys.at[step % 2, side], yr.at[step % 2, side], y_to[side])
+                      ys.at[side], yr.at[step % 2, side], y_to[side])
 
     def z_copy(step, side):
         src = p_hbm.at[0 if side == LO else planes - 1] if step == 0 else (
             fields[step % 2].at[1 if side == LO else planes])
         dst = fields[step % 2].at[planes + 1 if side == LO else 0]
-        return remote(src, dst, zs.at[step % 2, side], zr.at[step % 2, side], z_to[side])
+        return remote(src, dst, zs.at[side], zr.at[step % 2, side], z_to[side])
 
     def update(step, cell, q, low, high, copies=(), before_last=None):
         now, then = fields[step % 2], fields[(step + 1) % 2]
@@ -195,22 +196,49 @@
             stat[0, cell, part, :] = GUESS + shift
             stat[1, cell, part, :] = lax.rsqrt(square / count - shift * shift + EPS)
 
-    for side in order(0):
-        for q in range(tiles):
-            for copy in x_copies(0, side, q):
-                copy.start()
-    if colored:
-        @pl.when(color == 0)
-        def _():
-            pl.semaphore_wait(barrier, len(near))
-
-    for side in (LO, HI):
-        z_copy(0, side).start()
-        y_copy(0, side).start()
+    def start_cols():
+        for side in order(0):
+            for q in range(tiles):
+                for copy in x_copies(0, side, q):
+                    copy.start()
+
+    if paired:
+        pl.when(early)(start_cols)
+    else:
+        start_cols()
+    def swap_rows():
+        for side in (LO, HI):
+            z_copy(0, side).start()
+        for side in (LO, HI):
+            z_copy(0, side).wait_recv()
+
+    def start_early():
+        pl.semaphore_wait(barrier, len(y_to))
+        for side in (LO, HI):
+            y_copy(0, side).start()
+        pl.semaphore_wait(heard, len(y_to))
+        swap_rows()
+
+    def start_late():
+        for side in (LO, HI):
+            y_copy(0, side).start()
+        swap_rows()
+        for device in y_to:
+            pl.semaphore_signal(heard, inc=1, device_id=device, device_id_type=MESH)
+
     for load in loads:
         load.start()
+    if paired:
+        pl.when(early)(start_early)
+        pl.when(jnp.logical_not(early))(start_late)
+    else:
+        for side in (LO, HI):
+            y_copy(0, side).start()
+        swap_rows()
     for load in loads:
         load.wait()
+    if paired:
+        pl.when(jnp.logical_not(early))(start_cols)
 
     for step in range(STEPS):
         if step >= 1:
@@ -219,7 +247,8 @@
                 y_copy(step - 1, side).wait_send()
                 x_sent(step - 1, side)
         for side in (LO, HI):
-            z_copy(step, side).wait_recv()
+            if step >= 1:
+                z_copy(step, side).wait_recv()
             y_copy(step, side).wait_recv()
         interior(step)
         if step == STEPS - 1:
@@ -298,10 +327,11 @@
             pltpu.VMEM((STEPS, 2, planes, cells, TILE, members), jnp.float32),
             pltpu.VMEM((rows, cells, tiles, 2, TILE, members), jnp.float32),
             dma((2, 2)), dma((2, 2, tiles)), dma((PIECES,)),
-            dma((2, 2)), dma((2, 2)),
-            dma((2, 2)), dma((2, 2)),
+            dma((2,)), dma((2, 2)),
+            dma((2,)), dma((2, 2)),
             dma((rows - 1,)), dma((4, rows - 1)),
             dma((3,)),
+            pltpu.SemaphoreType.REGULAR,
         ],
         compiler_params=pltpu.CompilerParams(
             collective_id=0, has_side_effects=True, vmem_limit_bytes=46 * 1024 * 1024

time: 286 us -> 286 us (level)
  no operation moved by 1% of the time
where the time goes in v3:
time: 286 us
  Pallas kernels  285 us (100%)
    pallas_call x1, Pallas kernels, shards(): pl.pallas_call(functools.partial(leapfrog, sizes), out_shape=(pltpu.VMEM(...  279 us
    pallas_call x1, Pallas kernels, shards(): pl.pallas_call(rescale, out_shape=(jax.ShapeDtypeStruct(pressure.shape, j...  5.84 us

profile of v3, /device:TPU:1, one launch (start us, length us, event | category | flops | bytes accessed | tf_op | source)
XLA Modules:
  0.0 285.8 jit_solution(9956975095037623765)
XLA Ops:
  0.6 279.3 %shard_map.50 = (f32[128,4,32,128]{3,2,1,0:T(8,128)S(1)}, f32[2,4,32,128]{3,2,1,0:T(8,128)S(1)}) custom-call(f32[128,4,32,128]{3,2,1,0:T(8,128)} %p_hbm.1, f32[128,4,32,128]{3,2,1,0:T(8,128)} %e_hbm.1, f32[128,4,32,128]{3,2,1,0:T(8,128)} %s_hbm.1), custom_call_target="tpu_custom_call" | custom-call | tf_op jit(solution)/shard_map/pallas_call | solution.py:315
  279.9 5.8 %shard_map.51 = (f32[128,4,32,128]{3,2,1,0:T(8,128)}, f32[128,4,32,128]{3,2,1,0:T(8,128)}) custom-call(f32[128,4,32,128]{3,2,1,0:T(8,128)S(1)} %get-tuple-element.4.p_ref, f32[2,4,32,128]{3,2,1,0:T(8,128)S(1)} %get-tuple-element.5.stat_ref), custom_call_target="tpu_custom_call" | custom-call | tf_op jit(solution)/shard_map/pallas_call | solution.py:341

commit v4 on v3

--- a/solution.py
+++ b/solution.py
@@ -12,9 +12,17 @@
 EPS = 0.0001
 MESH = pl.DeviceIdType.MESH
 TILE = 8
-PIECES = 4
 PARTS = 8
 LO, HI = 0, 1
+
+
+def halving(planes):
+    spans, start = [], 0
+    while planes - start > TILE:
+        size = (planes - start) // (2 * TILE) * TILE
+        spans.append((start, size))
+        start += size
+    return spans + [(start, planes - start)]
 
 
 def leapfrog(sizes, p_hbm, e_hbm, s_hbm, end, stat,
@@ -101,8 +109,7 @@
     def x_copies(step, side, q):
         part = pl.ds(q * TILE, TILE)
         if step == STEPS - 1 and side == order(step)[1] and q == tiles - 1:
-            each = planes // PIECES
-            return [x_part(step, side, pl.ds(piece * each, each), part, xp.at[piece]) for piece in range(PIECES)]
+            return [x_part(step, side, pl.ds(*span), part, xp.at[i]) for i, span in enumerate(halving(planes))]
         return [x_part(step, side, slice(None), part, xr.at[step % 2, side, q])]
 
     def x_sent(step, side):
@@ -152,14 +159,13 @@
 
         zero = jnp.zeros((TILE, 128), jnp.float32)
         sums = (zero, zero) if last else 0
-        count_of = max(len(copies), 1)
-        blocks = planes // TILE // count_of
-        for i in range(count_of):
-            if before_last is not None and i == count_of - 1:
+        spans = halving(planes) if len(copies) > 1 else [(0, planes)]
+        for i, (start, size) in enumerate(spans):
+            if before_last is not None and i == len(spans) - 1:
                 before_last()
             if copies:
                 copies[i].wait_recv()
-            sums = lax.fori_loop(i * blocks, (i + 1) * blocks, block, sums)
+            sums = lax.fori_loop(start // TILE, (start + size) // TILE, block, sums)
         if last:
             line[row, cell, q, 0] = sums[0]
             line[row, cell, q, 1] = sums[1]
@@ -326,7 +332,7 @@
             pltpu.VMEM((STEPS, 2, planes, depth, members), jnp.float32),
             pltpu.VMEM((STEPS, 2, planes, cells, TILE, members), jnp.float32),
             pltpu.VMEM((rows, cells, tiles, 2, TILE, members), jnp.float32),
-            dma((2, 2)), dma((2, 2, tiles)), dma((PIECES,)),
+            dma((2, 2)), dma((2, 2, tiles)), dma((len(halving(planes)),)),
             dma((2,)), dma((2, 2)),
             dma((2,)), dma((2, 2)),
             dma((rows - 1,)), dma((4, rows - 1)),

time: 286 us -> 286 us (level)
  no operation moved by 1% of the time
where the time goes in v4:
time: 286 us
  Pallas kernels  285 us (100%)
    pallas_call x1, Pallas kernels, shards(): pl.pallas_call(functools.partial(leapfrog, sizes), out_shape=(pltpu.VMEM(...  279 us
    pallas_call x1, Pallas kernels, shards(): pl.pallas_call(rescale, out_shape=(jax.ShapeDtypeStruct(pressure.shape, j...  5.84 us

profile of v4, /device:TPU:1, one launch (start us, length us, event | category | flops | bytes accessed | tf_op | source)
XLA Modules:
  0.0 285.7 jit_solution(8326076591008336525)
XLA Ops:
  0.6 279.2 %shard_map.50 = (f32[128,4,32,128]{3,2,1,0:T(8,128)S(1)}, f32[2,4,32,128]{3,2,1,0:T(8,128)S(1)}) custom-call(f32[128,4,32,128]{3,2,1,0:T(8,128)} %p_hbm.1, f32[128,4,32,128]{3,2,1,0:T(8,128)} %e_hbm.1, f32[128,4,32,128]{3,2,1,0:T(8,128)} %s_hbm.1), custom_call_target="tpu_custom_call" | custom-call | tf_op jit(solution)/shard_map/pallas_call | solution.py:321
  279.8 5.8 %shard_map.51 = (f32[128,4,32,128]{3,2,1,0:T(8,128)}, f32[128,4,32,128]{3,2,1,0:T(8,128)}) custom-call(f32[128,4,32,128]{3,2,1,0:T(8,128)S(1)} %get-tuple-element.4.p_ref, f32[2,4,32,128]{3,2,1,0:T(8,128)S(1)} %get-tuple-element.5.stat_ref), custom_call_target="tpu_custom_call" | custom-call | tf_op jit(solution)/shard_map/pallas_call | solution.py:347

commit v5 on v4

--- a/solution.py
+++ b/solution.py
@@ -229,6 +229,7 @@
         for side in (LO, HI):
             y_copy(0, side).start()
         swap_rows()
+        start_cols()
         for device in y_to:
             pl.semaphore_signal(heard, inc=1, device_id=device, device_id_type=MESH)
 
@@ -243,8 +244,6 @@
         swap_rows()
     for load in loads:
         load.wait()
-    if paired:
-        pl.when(jnp.logical_not(early))(start_cols)
 
     for step in range(STEPS):
         if step >= 1:

time: 286 us -> 286 us (level)
  no operation moved by 1% of the time
where the time goes in v5:
time: 286 us
  Pallas kernels  285 us (100%)
    pallas_call x1, Pallas kernels, shards(): pl.pallas_call(functools.partial(leapfrog, sizes), out_shape=(pltpu.VMEM(...  279 us
    pallas_call x1, Pallas kernels, shards(): pl.pallas_call(rescale, out_shape=(jax.ShapeDtypeStruct(pressure.shape, j...  5.84 us

profile of v5, /device:TPU:1, one launch (start us, length us, event | category | flops | bytes accessed | tf_op | source)
XLA Modules:
  0.0 285.7 jit_solution(3444649154321620839)
XLA Ops:
  0.6 279.2 %shard_map.50 = (f32[128,4,32,128]{3,2,1,0:T(8,128)S(1)}, f32[2,4,32,128]{3,2,1,0:T(8,128)S(1)}) custom-call(f32[128,4,32,128]{3,2,1,0:T(8,128)} %p_hbm.1, f32[128,4,32,128]{3,2,1,0:T(8,128)} %e_hbm.1, f32[128,4,32,128]{3,2,1,0:T(8,128)} %s_hbm.1), custom_call_target="tpu_custom_call" | custom-call | tf_op jit(solution)/shard_map/pallas_call | solution.py:320
  279.8 5.8 %shard_map.51 = (f32[128,4,32,128]{3,2,1,0:T(8,128)}, f32[128,4,32,128]{3,2,1,0:T(8,128)}) custom-call(f32[128,4,32,128]{3,2,1,0:T(8,128)S(1)} %get-tuple-element.4.p_ref, f32[2,4,32,128]{3,2,1,0:T(8,128)S(1)} %get-tuple-element.5.stat_ref), custom_call_target="tpu_custom_call" | custom-call | tf_op jit(solution)/shard_map/pallas_call | solution.py:346
